TPU v7x, 32 devices: a whole 2x2x4 slice. The times are simulated.
32 devices in a mesh: fsdp: 2 (over y), tensor: 16 (over z, x, core).
Axes of the slice: x: 2, y: 2, z: 4, core: 2. Of those that a mesh axis runs over, the one named last changes fastest.
Arguments:
- momentum: bfloat16 [8192, 28672], P('fsdp', 'tensor'), may hold values from -6 to 6
- gradient: bfloat16 [8192, 28672], P('fsdp', 'tensor'), may hold values from -4 to 4
- factor: float32 [28672, 512], P('tensor', 'fsdp'), may hold values from -0.03125 to 0.03125
Outputs:
- new_momentum: bfloat16 [8192, 28672], P('fsdp', 'tensor')
- new_factor: float32 [28672, 512], P('tensor', 'fsdp')
- update: bfloat16 [8192, 28672], P('fsdp', 'tensor')
All inputs are finite; a program needn't handle non-finite values.
Results may differ from a plain program's by a relative error of at most 0.017.
Values may be sent and summed in bfloat16 or wider, within the bound.
A program may use at most 128 MiB of HBM per device.

v0:
```python
import jax
import jax.numpy as jnp
from jax import lax
from jax.sharding import PartitionSpec as P

D = 8192
FF = 28672
R = 512
decay_rate = 0.95
epsilon = 1e-06


def on_device(momentum, gradient, factor):
    blended = (momentum.astype(jnp.float32) + gradient.astype(jnp.float32)).astype(jnp.bfloat16)
    lowered = factor.astype(jnp.bfloat16)
    partial_left = jnp.dot(
        blended,
        lax.all_gather(lowered, "fsdp", axis=1, tiled=True),
        preferred_element_type=jnp.float32,
    )
    left_factor = lax.psum(partial_left, "tensor")
    local_gram = lax.dot_general(
        left_factor, left_factor, (((0,), (0,)), ((), ())), precision=lax.Precision.HIGHEST
    )
    gram_matrix = lax.psum(local_gram, "fsdp")
    lower_factor = jnp.linalg.cholesky(gram_matrix)
    solved = jax.scipy.linalg.solve_triangular(lower_factor, left_factor.T, lower=True)
    orthonormal = solved.T.astype(jnp.bfloat16)
    right_share = lax.psum_scatter(
        lax.dot_general(
            orthonormal, blended, (((0,), (0,)), ((), ())), preferred_element_type=jnp.float32
        ).astype(jnp.bfloat16),
        "fsdp",
        scatter_dimension=0,
        tiled=True,
    ).astype(jnp.float32)
    square_sums = lax.psum(jnp.sum(right_share * right_share, axis=1), "tensor")
    own_inverse = lax.rsqrt(square_sums + epsilon)
    own_factor = (right_share * own_inverse[:, None]).T
    right_rows, inverse = (
        lax.all_gather(right_share, "fsdp", axis=0, tiled=True),
        lax.all_gather(own_inverse, "fsdp", axis=0, tiled=True),
    )
    full_rows = right_rows * inverse[:, None]
    product = jnp.dot(
        orthonormal, right_rows.astype(jnp.bfloat16), preferred_element_type=jnp.float32
    )
    stepped = jnp.dot(
        orthonormal, full_rows.astype(jnp.bfloat16), preferred_element_type=jnp.float32
    )
    new_momentum = (blended.astype(jnp.float32) - (1.0 - decay_rate) * product).astype(jnp.bfloat16)
    update = (stepped * jnp.sqrt(jnp.float32(D * FF / R))).astype(jnp.bfloat16)
    return (new_momentum, own_factor, update)


def solution(mesh):
    placed = (P("fsdp", "tensor"), P("fsdp", "tensor"), P("tensor", "fsdp"))
    return jax.shard_map(
        on_device,
        mesh=mesh,
        in_specs=placed,
        out_specs=(P("fsdp", "tensor"), P("tensor", "fsdp"), P("fsdp", "tensor")),
        check_vma=False,
    )
```

profile of v0, /device:TPU:0, one launch (start us, length us, event | category | flops | bytes accessed | tf_op | source)
XLA Modules:
  0.0 598.9 jit_solution(7872715118207155491)
XLA Ops:
  7.2 2.5 convert_element_type.39
  9.8 33.1 %all-gather.4.cloned.1.call-done = bf16[1792,512]{1,0:T(8,128)(2,1)} async-done(((bf16[1792,256]{1,0:T(8,128)(2,1)}), bf16[1792,512]{1,0:T(8,128)(2,1)}) %all-gather.4.cloned.1.call-update) | async-done | bytes 1835024 | tf_op jit(solution)/shard_map/all_gather | solution.py:18
  42.9 15.9 %fusion.35 = f32[4096,512]{1,0:T(8,128)} fusion(bf16[1792,512]{1,0:T(8,128)(2,1)} %all-gather.4.cloned.1.call-done, bf16[4096,1792]{1,0:T(8,128)(2,1)} %param.4, bf16[4096,1792]{1,0:T(8,128)(2,1)} %param.3), kind=kOutput, calls=%fused_computation.77 | convolution fusion | flops 7545552896 | bytes 39583744 | tf_op jit(solution)/shard_map/dot_general | solution.py:16
  58.9 170.2 %all-reduce.4.cloned.1.call-done = f32[4096,512]{1,0:T(8,128)} async-done(((f32[4096,512]{1,0:T(8,128)}), f32[4096,512]{1,0:T(8,128)}) %all-reduce.4.cloned.1.call-update) | async-done | bytes 8388624 | tf_op jit(solution)/shard_map/psum | solution.py:21
  229.1 18.5 %fusion.40 = f32[512,512]{0,1:T(8,128)} fusion(f32[4096,512]{1,0:T(8,128)} %all-reduce.4.cloned.1.call-done), kind=kOutput, calls=%fused_computation.82 | convolution fusion | flops 12884901888 | bytes 9437184 | tf_op jit(solution)/shard_map/dot_general | solution.py:22
  247.6 0.5 reduce-scatter.2.cloned.1.call-start
  248.1 39.6 %all-reduce.6.cloned.1.call-done = f32[512,512]{0,1:T(8,128)} async-done(((f32[512,512]{0,1:T(8,128)}), f32[512,512]{0,1:T(8,128)}) %all-reduce.6.cloned.1.call-update) | async-done | bytes 1048592 | tf_op jit(solution)/shard_map/psum | solution.py:25
  287.7 1.6 copy.10
  289.2 1.4 fusion.16
  290.7 11.7 %cholesky.104 = f32[128,128]{1,0:T(8,128)S(1)} custom-call(f32[128,128]{1,0:T(8,128)S(1)} %cholesky.266), custom_call_target="Cholesky" | custom-call | tf_op jit(solution)/shard_map/jit(cholesky)/cholesky | solution.py:26
  302.4 9.8 %custom-call.31 = f32[1,128,128]{1,2,0:T(8,128)S(1)} custom-call(f32[1,128,128]{2,1,0:T(8,128)S(1)} %get-tuple-element.36), custom_call_target="InvertDiagBlocksLowerTriangular" | custom-call | tf_op jit(solution)/shard_map/jit(cholesky)/cholesky | solution.py:26
  313.1 11.7 %cholesky.217 = f32[128,128]{1,0:T(8,128)S(1)} custom-call(f32[128,128]{1,0:T(8,128)S(1)} %cholesky.270), custom_call_target="Cholesky" | custom-call | tf_op jit(solution)/shard_map/jit(cholesky)/cholesky | solution.py:26
  324.8 10.0 %custom-call.32 = f32[1,128,128]{1,2,0:T(8,128)S(1)} custom-call(f32[1,128,128]{2,1,0:T(8,128)S(1)} %get-tuple-element.33), custom_call_target="InvertDiagBlocksLowerTriangular" | custom-call | tf_op jit(solution)/shard_map/jit(cholesky)/cholesky | solution.py:26
  335.0 0.4 convolution_subtract_fusion.3
  335.4 11.7 %cholesky.238 = f32[128,128]{1,0:T(8,128)S(1)} custom-call(f32[128,128]{1,0:T(8,128)S(1)} %cholesky.275), custom_call_target="Cholesky" | custom-call | tf_op jit(solution)/shard_map/jit(cholesky)/cholesky | solution.py:26
  347.2 0.6 compare_reduce_fusion.1
  347.8 9.8 %custom-call.33 = f32[1,128,128]{1,2,0:T(8,128)S(1)} custom-call(f32[1,128,128]{2,1,0:T(8,128)S(1)} %get-tuple-element.30), custom_call_target="InvertDiagBlocksLowerTriangular" | custom-call | tf_op jit(solution)/shard_map/jit(cholesky)/cholesky | solution.py:26
  357.8 0.4 convolution_subtract_fusion.4
  358.2 11.7 %cholesky.255 = f32[128,128]{1,0:T(8,128)S(1)} custom-call(f32[128,128]{1,0:T(8,128)S(1)} %convolution_subtract_fusion.4), custom_call_target="Cholesky" | custom-call | tf_op jit(solution)/shard_map/jit(cholesky)/cholesky | solution.py:26
  370.0 0.7 compare_reduce_fusion
  370.6 0.6 compare_reduce_fusion.2
  373.8 0.5 select_select_fusion
  374.3 8.0 %while.1 = (s32[]{:T(128)}, f32[512,512]{1,0:T(8,128)S(1)}, s32[4,2]{0,1:T(2,128)S(1)}, f32[4,128,128]{2,1,0:T(8,128)S(1)}, s32[]{:T(128)}) while((s32[]{:T(128)}, f32[512,512]{1,0:T(8,128)S(1)}, s32[4,2]{0,1:T(2,128)S(1)}, f32[4,128,128]{2,1,0:T(8,128)S(1)}, s32[]{:T(128)}) %tuple.36), condition=%wide.while_cond, body=%wide.while_body.sunk | while | flops 2 | bytes 131189 | solution.py:27
  374.4 0.5 fusion.50
  374.9 1.4 bitcast_dynamic-update-slice_fusion.2
  376.4 0.5 fusion.50
  376.9 1.4 bitcast_dynamic-update-slice_fusion.2
  378.4 0.5 fusion.50
  378.9 1.4 bitcast_dynamic-update-slice_fusion.2
  380.4 0.5 fusion.50
  380.9 1.4 bitcast_dynamic-update-slice_fusion.2
  382.3 39.3 %custom-call.34 = f32[4,128,128]{1,2,0:T(8,128)S(1)} custom-call(f32[4,128,128]{2,1,0:T(8,128)S(1)} %get-tuple-element.10), custom_call_target="InvertDiagBlocksLowerTriangular" | custom-call | tf_op jit(solution)/shard_map/jit(_solve_triangular)/triangular_solve | solution.py:27
  421.7 3.7 fusion.39
  425.4 5.5 convolution_subtract_fusion.1
  430.9 3.0 fusion.38
  433.9 7.3 %convolution_subtract_fusion = f32[128,4096]{0,1:T(8,128)S(1)} fusion(f32[128,4096]{1,0:T(8,128)S(1)} %get-tuple-element.42, f32[128,4096]{1,0:T(8,128)S(1)} %get-tuple-element.44, f32[512,4096]{0,1:T(8,128)S(1)} %bitcast.66, f32[512,512]{1,0:T(8,128)S(1)} %get-tuple-element.107), kind=kOutput, calls=%fused_computation.11 | convolution fusion | flops 1612185600 | bytes 8519680 | tf_op jit(solution)/shard_map/jit(_solve_triangular)/triangular_solve | solution.py:27
  441.3 2.9 fusion.37
  444.2 10.8 %fusion.6 = f32[128,4096]{0,1:T(8,128)S(1)} fusion(f32[128,4096]{1,0:T(8,128)S(1)} %get-tuple-element.40, f32[128,4096]{1,0:T(8,128)S(1)} %get-tuple-element.42, f32[128,4096]{1,0:T(8,128)S(1)} %get-tuple-element.44, f32[512,4096]{0,1:T(8,128)S(1)} %bitcast.67, f32[512,512]{1,0:T(8,128)S(1)} %get-tuple-element.107), kind=kOutput, calls=%fused_computation.13 | convolution fusion | flops 2419589120 | bytes 10682368 | tf_op jit(solution)/shard_map/jit(_solve_triangular)/triangular_solve | solution.py:27
  455.0 1.9 convolution_convert_fusion
  456.9 16.1 %convolution_convert_fusion.1 = bf16[512,1792]{1,0:T(8,128)(2,1)} fusion(bf16[128,4096]{1,0:T(8,128)(2,1)S(1)} %convolution_convert_fusion, bf16[128,4096]{1,0:T(8,128)(2,1)} %get-tuple-element.39, bf16[128,4096]{1,0:T(8,128)(2,1)} %get-tuple-element.41, bf16[128,4096]{1,0:T(8,128)(2,1)S(1)} %get-tuple-element.43, bf16[4096,1792]{1,0:T(8,128)(2,1)} %param.4, ...), kind=kOutput, calls=%fused_computation.20 | convolution fusion | flops 7563247616 | bytes 35389440 | tf_op jit(solution)/shard_map/dot_general | solution.py:30
  473.1 29.1 %reduce-scatter.2.cloned.1.call-done = bf16[256,1792]{1,0:T(8,128)(2,1)} async-done(((bf16[512,1792]{1,0:T(8,128)(2,1)}), bf16[256,1792]{1,0:T(8,128)(2,1)}) %reduce-scatter.2.cloned.1.call-update) | async-done | bytes 917520 | tf_op jit(solution)/shard_map/reduce_scatter | solution.py:29
  502.2 2.6 convert_element_type.41
  505.1 33.0 %psum.23 = f32[256]{0:T(256)S(1)} all-reduce(f32[256]{0:T(256)S(1)} %multiply_reduce_fusion), channel_id=1, replica_groups=mesh['fsdp'=2,'tensor'=16] {'tensor'}, use_global_device_ids=true, to_apply=%region_12.13 | all-reduce | flops 256 | bytes 2048 | tf_op jit(solution)/shard_map/psum | solution.py:37
  538.3 1.7 copy.11
  540.0 4.4 all-gather
  544.4 11.5 %all-gather.6.cloned.1.call-done = f32[512,1792]{1,0:T(8,128)} async-done(((f32[256,1792]{1,0:T(8,128)}), f32[512,1792]{1,0:T(8,128)}) %all-gather.6.cloned.1.call-update) | async-done | bytes 3670032 | tf_op jit(solution)/shard_map/all_gather | solution.py:41
  555.9 22.5 %subtract_convert_fusion = bf16[4096,1792]{1,0:T(8,128)(2,1)} fusion(f32[512,1792]{1,0:T(8,128)} %all-gather.6.cloned.1.call-done, bf16[128,4096]{1,0:T(8,128)(2,1)} %copy-done.1, bf16[128,4096]{1,0:T(8,128)(2,1)} %get-tuple-element.39, bf16[128,4096]{1,0:T(8,128)(2,1)} %get-tuple-element.41, bf16[128,4096]{1,0:T(8,128)(2,1)} %copy-done.3, ...), kind=kOutput, calls=%fused_computation.3 | convolution fusion | flops 7592607744 | bytes 51904512 | tf_op jit(solution)/shard_map/dot_general | solution.py:45
  578.4 13.5 %multiply_convert_fusion = bf16[4096,1792]{1,0:T(8,128)(2,1)} fusion(f32[512,1792]{1,0:T(8,128)} %all-gather.6.cloned.1.call-done, f32[512]{0:T(512)S(1)} %bitcast.69, bf16[128,4096]{1,0:T(8,128)(2,1)S(1)} %copy-done.2, bf16[128,4096]{1,0:T(8,128)(2,1)} %get-tuple-element.39, bf16[128,4096]{1,0:T(8,128)(2,1)S(1)} %copy-done.5, ...), kind=kOutput, calls=%fused_computation.2 | convolution fusion | flops 7549485056 | bytes 22546432 | tf_op jit(solution)/shard_map/dot_general | solution.py:48
  (48 shorter events, 2.4 us)
Async XLA Ops:
  7.2 35.8 %all-gather.4.cloned.1.call-start = ((), (), s32[]{:S(2)}) async-start(), calls=%async_computation.1 | async-start | bytes 2752512 | tf_op jit(solution)/shard_map/all_gather | solution.py:18
  9.7 219.3 %all-reduce.4.cloned.1.call-start = ((), (), s32[]{:S(2)}) async-start(), calls=%async_computation.2 | async-start | bytes 16777216 | tf_op jit(solution)/shard_map/psum | solution.py:21
  58.8 228.8 %all-reduce.6.cloned.1.call-start = ((), (), s32[]{:S(2)}) async-start(), calls=%async_computation.3 | async-start | bytes 2097152 | tf_op jit(solution)/shard_map/psum | solution.py:25
  247.6 254.7 %reduce-scatter.2.cloned.1.call-start = ((), (), s32[]{:S(2)}) async-start(), calls=%async_computation.4 | async-start | bytes 2752512 | tf_op jit(solution)/shard_map/reduce_scatter | solution.py:29
  421.6 12.3 %slice-start = ((s8[8388608]{0:T(1024)(128)(4,1)}), s8[4194304]{0:T(1024)(128)(4,1)S(1)}, s32[]{:S(2)}) async-start(s8[8388608]{0:T(1024)(128)(4,1)} %bitcast.64), calls=%async_computation.6 | async-start | bytes 8388608
  425.3 31.6 %copy-start.3 = (bf16[128,4096]{1,0:T(8,128)(2,1)}, bf16[128,4096]{1,0:T(8,128)(2,1)S(1)}, u32[]{:S(2)}) copy-start(bf16[128,4096]{1,0:T(8,128)(2,1)S(1)} %get-tuple-element.43) | copy-start | bytes 3145732
  425.4 8.6 %slice-start.1 = ((s8[8388608]{0:T(1024)(128)(4,1)}), s8[4194304]{0:T(1024)(128)(4,1)S(1)}, s32[]{:S(2)}) async-start(s8[8388608]{0:T(1024)(128)(4,1)} %bitcast.64), calls=%async_computation.7 | async-start | bytes 8388608
  456.9 16.1 %copy-start.1 = (bf16[128,4096]{1,0:T(8,128)(2,1)}, bf16[128,4096]{1,0:T(8,128)(2,1)S(1)}, u32[]{:S(2)}) copy-start(bf16[128,4096]{1,0:T(8,128)(2,1)S(1)} %convolution_convert_fusion) | copy-start | bytes 3145732
  473.0 82.8 %all-gather.6.cloned.1.call-start = ((), (), s32[]{:S(2)}) async-start(), calls=%async_computation.5 | async-start | bytes 5505024 | tf_op jit(solution)/shard_map/all_gather | solution.py:41
  502.2 2.6 copy-start
  544.4 34.0 %copy-start.2 = (bf16[128,4096]{1,0:T(8,128)(2,1)S(1)}, bf16[128,4096]{1,0:T(8,128)(2,1)}, u32[]{:S(2)}) copy-start(bf16[128,4096]{1,0:T(8,128)(2,1)} %copy-done.1) | copy-start | bytes 3145732
  544.4 34.0 %copy-start.4 = (bf16[128,4096]{1,0:T(8,128)(2,1)S(1)}, bf16[128,4096]{1,0:T(8,128)(2,1)}, u32[]{:S(2)}) copy-start(bf16[128,4096]{1,0:T(8,128)(2,1)} %copy-done.3) | copy-start | bytes 3145732
  544.4 34.0 %copy-start.5 = (bf16[128,4096]{1,0:T(8,128)(2,1)S(1)}, bf16[128,4096]{1,0:T(8,128)(2,1)}, u32[]{:S(2)}) copy-start(bf16[128,4096]{1,0:T(8,128)(2,1)} %get-tuple-element.41) | copy-start | bytes 3145732
Sparse Core Ops, SparseCore 0:
  10.1 32.8 all-gather.3
  59.0 170.0 all-reduce.3
  247.7 39.9 all-reduce.5
  473.2 29.0 reduce-scatter.1
  505.0 50.8 all-gather.5
where the time goes:
time: 605 us; the launch traced here: 599 us
  waiting for transfers between devices  284 us (47%)
  other arithmetic  125 us (21%)
  matrix products  124 us (20%)
  blocking collectives  37.4 us (6%)
  between operations  17 us (3%)
  local copies, waits for them, and re-layouts  11.3 us (2%)
    psum x1, waiting for transfers between devices, on_device(): left_factor = lax.psum(partial_left, 'tensor')  170 us
    another operation x14, other arithmetic, on_device(): lower_factor = jnp.linalg.cholesky(gram_matrix)  78.5 us
    another operation x3, other arithmetic, on_device(): jax.scipy.linalg.solve_triangular(lower_factor, left_factor.T, lower=True)  39.9 us
    psum x1, waiting for transfers between devices, on_device(): gram_matrix = lax.psum(local_gram, 'fsdp')  39.6 us
    another operation x7, matrix products, on_device(): jax.scipy.linalg.solve_triangular(lower_factor, left_factor.T, lower=True)  35.2 us
    all_gather x1, waiting for transfers between devices, on_device(): lax.all_gather(lowered, 'fsdp', axis=1, tiled=True)  33.1 us
    psum x1, blocking collectives, on_device(): square_sums = lax.psum(jnp.sum(right_share * right_share, axis=1), 'tensor')  33 us
    reduce_scatter x1, waiting for transfers between devices, on_device(): lax.psum_scatter(lax.dot_general(orthonormal, blended, (((0,), (0,)), (()...  29.1 us
  transfers between devices with their start and end apart: 5, of which 5 were waited for; matrix products, arithmetic and copies ran while one was open for 0% of the time, Pallas kernels for 0%

commit v1 on v0

--- a/solution.py
+++ b/solution.py
@@ -18,7 +18,11 @@
         lax.all_gather(lowered, "fsdp", axis=1, tiled=True),
         preferred_element_type=jnp.float32,
     )
-    left_factor = lax.psum(partial_left, "tensor")
+    left_factor = partial_left
+    for hop in (1, 2, 4, 8):
+        left_factor = left_factor + lax.ppermute(
+            left_factor, "tensor", [(dev, dev ^ hop) for dev in range(16)]
+        )
     local_gram = lax.dot_general(
         left_factor, left_factor, (((0,), (0,)), ((), ())), precision=lax.Precision.HIGHEST
     )

time: 605 us -> 1220 us (2.02)
  waiting for transfers between devices: 284 us -> 834 us
  other arithmetic: 125 us -> 173 us
    ppermute x0 -> x4, waiting for transfers between devices: none -> 734 us  [on_device(): lax.ppermute(left_factor, 'tensor', [(dev, dev ^ hop) for dev in range(16)])]
    psum x1 -> x0, waiting for transfers between devices: 170 us -> none  [on_device(): left_factor = lax.psum(partial_left, 'tensor')]
    add x0 -> x3, other arithmetic: none -> 33.8 us  [on_device(): left_factor + lax.ppermute(left_factor, 'tensor', [(dev, dev ^ hop) for d...]
  transfers between devices with their start and end apart: 5 -> 8, of which waited for: 5 -> 8; matrix products, arithmetic and copies ran while one was open for 0% -> 1% of each run, Pallas kernels for 0% -> 0%
where the time goes in v1:
time: 1220 us; the launch traced here: 1210 us
  waiting for transfers between devices  834 us (68%)
  other arithmetic  173 us (14%)
  matrix products  126 us (10%)
  blocking collectives  37.4 us (3%)
  between operations  17 us (1%)
  local copies, waits for them, and re-layouts  14.4 us (1%)
    ppermute x4, waiting for transfers between devices, on_device(): lax.ppermute(left_factor, 'tensor', [(dev, dev ^ hop) for dev in range(16)])  734 us
    another operation x14, other arithmetic, on_device(): lower_factor = jnp.linalg.cholesky(gram_matrix)  79 us
    another operation x3, other arithmetic, on_device(): jax.scipy.linalg.solve_triangular(lower_factor, left_factor.T, lower=True)  39.4 us
    add x3, other arithmetic, on_device(): left_factor + lax.ppermute(left_factor, 'tensor', [(dev, dev ^ hop) for d...  33.8 us
    all_gather x1, waiting for transfers between devices, on_device(): lax.all_gather(lowered, 'fsdp', axis=1, tiled=True)  33.1 us
    another operation x7, matrix products, on_device(): jax.scipy.linalg.solve_triangular(lower_factor, left_factor.T, lower=True)  33.1 us
    psum x1, blocking collectives, on_device(): square_sums = lax.psum(jnp.sum(right_share * right_share, axis=1), 'tensor')  33 us
    reduce_scatter x1, waiting for transfers between devices, on_device(): lax.psum_scatter(lax.dot_general(orthonormal, blended, (((0,), (0,)), (()...  29.1 us
  transfers between devices with their start and end apart: 8, of which 8 were waited for; matrix products, arithmetic and copies ran while one was open for 1% of the time, Pallas kernels for 0%

profile of v1, /device:TPU:0, one launch (start us, length us, event | category | flops | bytes accessed | tf_op | source)
XLA Modules:
  0.0 1207.9 jit_solution(17777514073994672508)
XLA Ops:
  7.2 2.5 convert_element_type.39
  9.8 33.1 %all-gather.4.cloned.1.call-done = bf16[1792,512]{1,0:T(8,128)(2,1)} async-done(((bf16[1792,256]{1,0:T(8,128)(2,1)}), bf16[1792,512]{1,0:T(8,128)(2,1)}) %all-gather.4.cloned.1.call-update) | async-done | bytes 1835024 | tf_op jit(solution)/shard_map/all_gather | solution.py:18
  42.9 13.7 %fusion.36 = f32[4096,512]{1,0:T(8,128)S(1)} fusion(bf16[1792,512]{1,0:T(8,128)(2,1)} %all-gather.4.cloned.1.call-done, bf16[4096,1792]{1,0:T(8,128)(2,1)} %param.4, bf16[4096,1792]{1,0:T(8,128)(2,1)} %param.3), kind=kOutput, calls=%fused_computation.82 | convolution fusion | flops 7545552896 | bytes 39583744 | tf_op jit(solution)/shard_map/dot_general | solution.py:16
  56.7 3.4 copy-done
  60.1 13.3 %collective-permute-done = f32[4096,512]{1,0:T(8,128)} collective-permute-done((f32[4096,512]{1,0:T(8,128)S(1)}, f32[4096,512]{1,0:T(8,128)}, u32[]{:S(2)}, u32[]{:S(2)}) %collective-permute-start) | collective-permute-done | bytes 8388640 | tf_op jit(solution)/shard_map/ppermute | solution.py:23
  73.3 11.3 add.69
  84.6 1.5 collective-permute-start.1
  86.1 181.3 %collective-permute-done.1 = f32[4096,512]{1,0:T(8,128)} collective-permute-done((f32[4096,512]{1,0:T(8,128)}, f32[4096,512]{1,0:T(8,128)}, u32[]{:S(2)}, u32[]{:S(2)}) %collective-permute-start.1) | collective-permute-done | bytes 8388640 | tf_op jit(solution)/shard_map/ppermute | solution.py:23
  267.4 11.3 add.70
  278.7 1.5 collective-permute-start.2
  280.2 180.5 %collective-permute-done.2 = f32[4096,512]{1,0:T(8,128)} collective-permute-done((f32[4096,512]{1,0:T(8,128)}, f32[4096,512]{1,0:T(8,128)}, u32[]{:S(2)}, u32[]{:S(2)}) %collective-permute-start.2) | collective-permute-done | bytes 8388640 | tf_op jit(solution)/shard_map/ppermute | solution.py:23
  460.6 11.3 add.71
  471.9 2.4 collective-permute-start.3
  474.3 359.4 %collective-permute-done.3 = f32[4096,512]{1,0:T(8,128)} collective-permute-done((f32[4096,512]{1,0:T(8,128)}, f32[4096,512]{1,0:T(8,128)}, u32[]{:S(2)}, u32[]{:S(2)}) %collective-permute-start.3) | collective-permute-done | bytes 8388640 | tf_op jit(solution)/shard_map/ppermute | solution.py:23
  833.7 25.7 %fusion.10 = f32[512,512]{0,1:T(8,128)} fusion(f32[4096,512]{1,0:T(8,128)} %add.71, f32[4096,512]{1,0:T(8,128)} %collective-permute-done.3), kind=kOutput, calls=%fused_computation.18 | convolution fusion | flops 12886999040 | bytes 17825792 | tf_op jit(solution)/shard_map/dot_general | solution.py:26
  859.8 11.6 add_bitcast_fusion
  871.4 28.2 %all-reduce.3.cloned.1.call-done = f32[512,512]{0,1:T(8,128)} async-done(((f32[512,512]{0,1:T(8,128)}), f32[512,512]{0,1:T(8,128)}) %all-reduce.3.cloned.1.call-update) | async-done | bytes 1048592 | tf_op jit(solution)/shard_map/psum | solution.py:29
  899.6 1.6 copy.10
  901.2 1.4 fusion.18
  902.6 11.7 cholesky.104
  914.4 9.8 custom-call.31
  925.0 11.9 cholesky.217
  936.9 9.8 custom-call.32
  947.4 11.7 cholesky.238
  959.8 9.8 custom-call.33
  970.2 12.1 %cholesky.255 = f32[128,128]{1,0:T(8,128)S(1)} custom-call(f32[128,128]{1,0:T(8,128)S(1)} %convolution_subtract_fusion.2), custom_call_target="Cholesky" | custom-call | tf_op jit(solution)/shard_map/jit(cholesky)/cholesky | solution.py:30
  986.3 7.7 while.1
  986.9 1.3 bitcast_dynamic-update-slice_fusion.2
  988.9 1.3 bitcast_dynamic-update-slice_fusion.2
  994.0 39.3 %custom-call.34 = f32[4,128,128]{1,2,0:T(8,128)S(1)} custom-call(f32[4,128,128]{2,1,0:T(8,128)S(1)} %get-tuple-element.10), custom_call_target="InvertDiagBlocksLowerTriangular" | custom-call | tf_op jit(solution)/shard_map/jit(_solve_triangular)/triangular_solve | solution.py:31
  1033.3 4.5 fusion.40
  1037.8 3.5 fusion.27
  1041.3 3.7 fusion.39
  1045.1 7.1 fusion.6
  1052.2 2.1 fusion.38
  1054.3 10.2 fusion
  1064.5 2.0 convolution_convert_fusion
  1066.6 15.8 %convolution_convert_fusion.1 = bf16[512,1792]{1,0:T(8,128)(2,1)} fusion(bf16[128,4096]{1,0:T(8,128)(2,1)S(1)} %convolution_convert_fusion, bf16[128,4096]{1,0:T(8,128)(2,1)S(1)} %get-tuple-element.39, bf16[128,4096]{1,0:T(8,128)(2,1)S(1)} %get-tuple-element.41, bf16[128,4096]{1,0:T(8,128)(2,1)} %get-tuple-element.43, bf16[4096,1792]{1,0:T(8,128)(2,1)} %param.4, ...), kind=kOutput, calls=%fused_computation.21 | convolution fusion | flops 7563247616 | bytes 35389440 | tf_op jit(solution)/shard_map/dot_general | solution.py:34
  1082.4 29.1 %reduce-scatter.2.cloned.1.call-done = bf16[256,1792]{1,0:T(8,128)(2,1)} async-done(((bf16[512,1792]{1,0:T(8,128)(2,1)}), bf16[256,1792]{1,0:T(8,128)(2,1)}) %reduce-scatter.2.cloned.1.call-update) | async-done | bytes 917520 | tf_op jit(solution)/shard_map/reduce_scatter | solution.py:33
  1111.6 2.5 convert_element_type.41
  1114.1 1.4 multiply_reduce_fusion
  1115.5 33.0 %psum.15 = f32[256]{0:T(256)S(1)} all-reduce(f32[256]{0:T(256)S(1)} %multiply_reduce_fusion), channel_id=1, replica_groups=mesh['fsdp'=2,'tensor'=16] {'tensor'}, use_global_device_ids=true, to_apply=%region_11.12 | all-reduce | flops 256 | bytes 2048 | tf_op jit(solution)/shard_map/psum | solution.py:41
  1148.5 1.4 multiply_bitcast_fusion
  1149.9 1.7 copy.11
  1151.6 4.4 all-gather
  1156.0 9.1 all-gather.6.cloned.1.call-done
  1165.1 22.4 %subtract_convert_fusion = bf16[4096,1792]{1,0:T(8,128)(2,1)} fusion(f32[512,1792]{1,0:T(8,128)} %all-gather.6.cloned.1.call-done, bf16[128,4096]{1,0:T(8,128)(2,1)} %copy-done.4, bf16[128,4096]{1,0:T(8,128)(2,1)} %copy-done.1, bf16[128,4096]{1,0:T(8,128)(2,1)S(1)} %get-tuple-element.41, bf16[128,4096]{1,0:T(8,128)(2,1)} %get-tuple-element.43, ...), kind=kOutput, calls=%fused_computation.3 | convolution fusion | flops 7592607744 | bytes 51904512 | tf_op jit(solution)/shard_map/dot_general | solution.py:49
  1187.5 13.5 %multiply_convert_fusion = bf16[4096,1792]{1,0:T(8,128)(2,1)} fusion(f32[512,1792]{1,0:T(8,128)} %all-gather.6.cloned.1.call-done, f32[512]{0:T(512)S(1)} %bitcast.61, bf16[128,4096]{1,0:T(8,128)(2,1)} %copy-done.4, bf16[128,4096]{1,0:T(8,128)(2,1)S(1)} %copy-done.2, bf16[128,4096]{1,0:T(8,128)(2,1)S(1)} %get-tuple-element.41, ...), kind=kOutput, calls=%fused_computation.2 | convolution fusion | flops 7549485056 | bytes 22546432 | tf_op jit(solution)/shard_map/dot_general | solution.py:52
  (55 shorter events, 9.9 us)
Async XLA Ops:
  7.2 35.8 %all-gather.4.cloned.1.call-start = ((), (), s32[]{:S(2)}) async-start(), calls=%async_computation.1 | async-start | bytes 2752512 | tf_op jit(solution)/shard_map/all_gather | solution.py:18
  9.7 889.9 %all-reduce.3.cloned.1.call-start = ((), (), s32[]{:S(2)}) async-start(), calls=%async_computation.2 | async-start | bytes 2097152 | tf_op jit(solution)/shard_map/psum | solution.py:29
  56.7 3.4 copy-start
  60.1 13.3 %collective-permute-start = (f32[4096,512]{1,0:T(8,128)S(1)}, f32[4096,512]{1,0:T(8,128)}, u32[]{:S(2)}, u32[]{:S(2)}) collective-permute-start(f32[4096,512]{1,0:T(8,128)S(1)} %fusion.36), channel_id=1, source_target_pairs={{0,1},{1,0},{2,3},{3,2},{4,5},{5,4},{6,7},{7,6},{8,9},{9,8},{10,11... | collective-permute-start | bytes 25165832 | tf_op jit(solution)/shard_map/ppermute | solution.py:23
  84.6 182.8 %collective-permute-start.1 = (f32[4096,512]{1,0:T(8,128)}, f32[4096,512]{1,0:T(8,128)}, u32[]{:S(2)}, u32[]{:S(2)}) collective-permute-start(f32[4096,512]{1,0:T(8,128)} %add.69), channel_id=1, source_target_pairs={{0,2},{1,3},{2,0},{3,1},{4,6},{5,7},{6,4},{7,5},{8,10},{9,11},{10,... | collective-permute-start | bytes 25165832 | tf_op jit(solution)/shard_map/ppermute | solution.py:23
  278.7 182.0 %collective-permute-start.2 = (f32[4096,512]{1,0:T(8,128)}, f32[4096,512]{1,0:T(8,128)}, u32[]{:S(2)}, u32[]{:S(2)}) collective-permute-start(f32[4096,512]{1,0:T(8,128)} %add.70), channel_id=1, source_target_pairs={{0,4},{1,5},{2,6},{3,7},{4,0},{5,1},{6,2},{7,3},{8,12},{9,13},{10,... | collective-permute-start | bytes 25165832 | tf_op jit(solution)/shard_map/ppermute | solution.py:23
  471.9 361.8 %collective-permute-start.3 = (f32[4096,512]{1,0:T(8,128)}, f32[4096,512]{1,0:T(8,128)}, u32[]{:S(2)}, u32[]{:S(2)}) collective-permute-start(f32[4096,512]{1,0:T(8,128)} %add.71), channel_id=1, source_target_pairs={{0,8},{1,9},{2,10},{3,11},{4,12},{5,13},{6,14},{7,15},{8,0},{9,1},... | collective-permute-start | bytes 25165832 | tf_op jit(solution)/shard_map/ppermute | solution.py:23
  859.4 252.2 %reduce-scatter.2.cloned.1.call-start = ((), (), s32[]{:S(2)}) async-start(), calls=%async_computation.3 | async-start | bytes 2752512 | tf_op jit(solution)/shard_map/reduce_scatter | solution.py:33
  1037.8 14.4 %slice-start = ((s8[8388608]{0:T(1024)(128)(4,1)}), s8[4194304]{0:T(1024)(128)(4,1)S(1)}, s32[]{:S(2)}) async-start(s8[8388608]{0:T(1024)(128)(4,1)} %bitcast.58), calls=%async_computation.5 | async-start | bytes 8388608
  1041.3 10.9 slice-start.1
  1054.3 12.3 %copy-start.1 = (bf16[128,4096]{1,0:T(8,128)(2,1)}, bf16[128,4096]{1,0:T(8,128)(2,1)S(1)}, u32[]{:S(2)}) copy-start(bf16[128,4096]{1,0:T(8,128)(2,1)S(1)} %get-tuple-element.39) | copy-start | bytes 3145732
  1066.6 15.8 %copy-start.4 = (bf16[128,4096]{1,0:T(8,128)(2,1)}, bf16[128,4096]{1,0:T(8,128)(2,1)S(1)}, u32[]{:S(2)}) copy-start(bf16[128,4096]{1,0:T(8,128)(2,1)S(1)} %convolution_convert_fusion) | copy-start | bytes 3145732
  1082.4 82.7 %all-gather.6.cloned.1.call-start = ((), (), s32[]{:S(2)}) async-start(), calls=%async_computation.4 | async-start | bytes 5505024 | tf_op jit(solution)/shard_map/all_gather | solution.py:45
  1156.0 31.5 %copy-start.2 = (bf16[128,4096]{1,0:T(8,128)(2,1)S(1)}, bf16[128,4096]{1,0:T(8,128)(2,1)}, u32[]{:S(2)}) copy-start(bf16[128,4096]{1,0:T(8,128)(2,1)} %copy-done.1) | copy-start | bytes 3145732
  1156.0 31.5 %copy-start.3 = (bf16[128,4096]{1,0:T(8,128)(2,1)S(1)}, bf16[128,4096]{1,0:T(8,128)(2,1)}, u32[]{:S(2)}) copy-start(bf16[128,4096]{1,0:T(8,128)(2,1)} %get-tuple-element.43) | copy-start | bytes 3145732
Sparse Core Ops, SparseCore 0:
  10.1 32.8 all-gather.3
  859.5 40.0 all-reduce.2
  1082.5 29.0 reduce-scatter.1
  1114.2 50.8 all-gather.5
